TPU v7x, 256 devices: a whole 4x4x8 slice. The times are simulated.
256 devices in a mesh: seq: 16 (over z, core), grp: 2 (over y_hi), dp: 8 (over y_lo, x).
Axes of the slice: x: 4, y: 4 (y_hi: 2, y_lo: 2; y = y_hi * 2 + y_lo), z: 8, core: 2. Of those that a mesh axis runs over, the one named last changes fastest.
Arguments:
- clips: bfloat16 [8, 2048, 1408], P('dp', 'seq'), may hold values from -6 to 6
- context: int32 [8, 2048], P('dp', 'seq'), may hold values from 0 to 1, as said below
- predict_index: int32 [8, 3072], P('dp', 'seq'), may hold values from -1 to 2047, as said below
- target_qkv: bfloat16 [3, 1408, 1408], P(None, 'dp', 'grp'), may hold values from -8 to 8
- target_out: bfloat16 [1408, 1408], P('grp'), may hold values from -0.15625 to 0.15625
- student_qkv: bfloat16 [3, 1408, 1408], P(None, 'dp', 'grp'), may hold values from -8 to 8
- student_out: bfloat16 [1408, 1408], P('grp', 'dp'), may hold values from -0.15625 to 0.15625
- mask_token: float32 [1408], replicated, may hold values from -4 to 4
Outputs:
- out_grad: float32 [1408, 1408], P('grp', 'dp')
- target_blend: float32 [1408, 1408], P('grp')
Inputs may be any that keep to these rules, and one draw needn't show every extreme that they name: In every aligned block of 128 tokens of a clip exactly 32 tokens have context 1 and the others 0. `predict_index`: each device's 192 slots name distinct target positions (context 0) of its clip, followed by -1 in the unused slots; different devices' lists may name the same position. In every clip one list is full.
All inputs are finite; a program needn't handle non-finite values.
Results may differ from a plain program's by a relative error of at most 0.014.
Values may be sent and summed in bfloat16 or wider, within the bound.
No kernel may reach another device: no remote copies, remote signals or barrier semaphores. Data moves between devices by JAX's collectives and lax.ppermute only.
A program may use at most 128 MiB of HBM per device.

v0:
```python
import math
import jax
import jax.numpy as jnp
from jax import lax
from jax.sharding import PartitionSpec as P

HEAD_DIM = 88
CTX_DEV = 32
EPSILON = 1e-06
MOMENTUM = 0.99


def side_by_side(arrays, axis, dim, along):
    ends, at = ([], 0)
    for a in arrays[:-1]:
        at += a.shape[along]
        ends.append(at)
    both = jnp.concatenate(arrays, axis=along)
    return tuple(jnp.split(lax.all_gather(both, axis, axis=dim, tiled=True), ends, axis=along))


def from_everyone(shard, axis):
    copies = jnp.broadcast_to(shard, (lax.axis_size(axis), *shard.shape))
    return lax.all_to_all(copies, axis, split_axis=0, concat_axis=0, tiled=True)


def taken_together(shard, axis):
    return from_everyone(shard, axis).astype(jnp.float32).sum(axis=0)


def in_order(tiles, dim):
    shape = list(tiles.shape[1:])
    shape[dim] *= tiles.shape[0]
    return jnp.moveaxis(tiles, 0, dim).reshape(shape)


def collect(shard, axis, dim):
    return in_order(from_everyone(shard, axis), dim)


def total_of_pieces(shard, axis):
    return lax.all_gather(shard, axis).astype(jnp.float32).sum(0)


def layer_norm(values):
    center = values - jnp.mean(values, axis=-1, keepdims=True)
    factor = lax.rsqrt(jnp.mean(center * center, axis=-1, keepdims=True) + EPSILON)
    return (center * factor, factor)


def position_table(places, width):
    half_width = width // 2
    spacing = jnp.exp(jnp.arange(half_width, dtype=jnp.float32) * (-math.log(10000.0) / half_width))
    angles = places.astype(jnp.float32)[:, None] * spacing[None, :]
    return jnp.concatenate([jnp.sin(angles), jnp.cos(angles)], axis=1)


def to_heads(queries):
    head_count = queries.shape[1] // HEAD_DIM
    return queries.reshape(queries.shape[0], head_count, HEAD_DIM).transpose(1, 0, 2)


def empty_state(head_count, row_count):
    peaks = jnp.full((head_count, row_count), -1e30, jnp.float32)
    totals = jnp.zeros((head_count, row_count), jnp.float32)
    summed = jnp.zeros((head_count, row_count, HEAD_DIM), jnp.float32)
    return (peaks, totals, summed)


def from_heads(running):
    peaks, totals, summed = running
    mixed = summed / totals[:, :, None]
    head_count, row_count, unused = mixed.shape
    return mixed.transpose(1, 0, 2).reshape(row_count, head_count * HEAD_DIM).astype(jnp.bfloat16)


def attend_shard(running, shard_rows, query_heads):
    peaks, totals, summed = running
    key_rows, value_rows = shard_rows
    length = key_rows.shape[0]
    head_count = query_heads.shape[0]
    key_heads = key_rows.reshape(length, head_count, HEAD_DIM)
    value_heads = value_rows.reshape(length, head_count, HEAD_DIM)
    factor = HEAD_DIM ** (-0.5)
    scores = (
        jnp.einsum("hqd,khd->hqk", query_heads, key_heads, preferred_element_type=jnp.float32)
        * factor
    )
    raised = jnp.maximum(peaks, jnp.max(scores, axis=2))
    shifted = jnp.exp(scores - raised[:, :, None])
    totals = jnp.sum(shifted, axis=2)
    summed = jnp.einsum(
        "hqk,khd->hqd",
        shifted.astype(jnp.bfloat16),
        value_heads,
        preferred_element_type=jnp.float32,
    )
    return (raised, totals, summed)


def body(
    clips, context, predict_index, target_qkv, target_out, student_qkv, student_out, mask_token
):
    tokens = clips[0]
    keep_flags = context[0]
    listed = predict_index[0]
    row_count, width = tokens.shape
    half_width = target_qkv.shape[2]
    head_count = half_width // HEAD_DIM
    normed = layer_norm(tokens.astype(jnp.float32))[0].astype(jnp.bfloat16)
    projected = jnp.einsum(
        "nr,krc->knc",
        normed,
        lax.all_gather(target_qkv, "dp", axis=1, tiled=True),
        preferred_element_type=jnp.float32,
    )
    projected = projected.astype(jnp.bfloat16)
    target_state = attend_shard(
        empty_state(head_count, row_count),
        side_by_side((projected[1], projected[2]), "seq", 0, 1),
        query_heads=to_heads(projected[0]),
    )
    target_mixed = from_heads(target_state)
    target_part = jnp.dot(target_mixed, target_out, preferred_element_type=jnp.float32)
    target_sum = taken_together(target_part.astype(jnp.bfloat16), "grp").astype(jnp.float32)
    features = layer_norm(tokens.astype(jnp.float32) + target_sum)[0].astype(jnp.bfloat16)
    first_row = lax.axis_index("seq") * row_count
    every_list = lax.all_gather(listed, "seq", axis=0, tiled=True)
    places = first_row + jnp.arange(row_count, dtype=jnp.int32)
    usable = jnp.sum((every_list[None, :] == places[:, None]).astype(jnp.float32), axis=1)
    slot_count = places.shape[0]
    is_context = keep_flags == 1
    context_order = jnp.cumsum(is_context.astype(jnp.int32)) - 1
    selector = (
        (context_order[None, :] == jnp.arange(CTX_DEV, dtype=jnp.int32)[:, None])
        & is_context[None, :]
    ).astype(jnp.bfloat16)
    context_rows = jnp.dot(selector, normed, preferred_element_type=jnp.float32).astype(
        jnp.bfloat16
    )
    seeds = mask_token[None, :] + position_table(jnp.maximum(places, 0), width)
    seed_normed = layer_norm(seeds)[0].astype(jnp.bfloat16)
    shard_rows = lax.all_gather(student_qkv, "dp", axis=1, tiled=True)
    query_total = jnp.dot(seed_normed, shard_rows[0], preferred_element_type=jnp.float32)
    pair_total = jnp.einsum(
        "nr,krc->knc", context_rows, shard_rows[1:], preferred_element_type=jnp.float32
    )
    student_pairs = pair_total
    student_pairs = student_pairs.astype(jnp.bfloat16)
    student_state = attend_shard(
        empty_state(head_count, slot_count),
        side_by_side((student_pairs[0], student_pairs[1]), "seq", 0, 1),
        query_heads=to_heads(query_total.astype(jnp.bfloat16)),
    )
    student_mixed = from_heads(student_state)
    relaid = collect(student_out, "dp", 1)
    student_part = jnp.dot(student_mixed, relaid, preferred_element_type=jnp.float32)
    student_sum = taken_together(student_part.astype(jnp.bfloat16), "grp").astype(jnp.float32)
    predicted, factor = layer_norm(seeds + student_sum)
    wanted = features.astype(jnp.float32)
    slope = jnp.clip(predicted - wanted, -1.0, 1.0) * usable[:, None]
    back_grad = (
        slope
        - jnp.mean(slope, axis=1, keepdims=True)
        - predicted * jnp.mean(slope * predicted, axis=1, keepdims=True)
    ) * factor
    arrived_grad = lax.all_to_all(
        back_grad.astype(jnp.bfloat16), "dp", split_axis=1, concat_axis=0, tiled=True
    ).astype(back_grad.dtype)
    column_grad = jnp.dot(
        collect(student_mixed, "dp", 0).astype(jnp.float32).T,
        arrived_grad,
        precision=lax.Precision.HIGHEST,
    )
    out_grad = total_of_pieces(column_grad.astype(jnp.bfloat16), "seq").astype(jnp.float32)
    target_blend = MOMENTUM * target_out.astype(jnp.float32) + (1.0 - MOMENTUM) * relaid.astype(
        jnp.float32
    )
    return (out_grad, target_blend)


def solution(mesh):
    in_specs = (
        P("dp", "seq", None),
        P("dp", "seq"),
        P("dp", "seq"),
        P(None, "dp", "grp"),
        P("grp", None),
        P(None, "dp", "grp"),
        P("grp", "dp"),
        P(),
    )
    out_specs = (P("grp", "dp"), P("grp", None))
    return jax.shard_map(body, mesh=mesh, in_specs=in_specs, out_specs=out_specs, check_vma=False)
```

profile of v0, /device:TPU:1, one launch (start us, length us, event | category | flops | bytes accessed | tf_op | source)
XLA Modules:
  0.0 378.8 jit_solution(2084272642977128158)
XLA Ops:
  7.2 0.7 all-gather.9.cloned.1.call-update
  7.9 0.7 all-gather.13.cloned.1.call-update
  8.7 0.7 compare_bitcast_fusion
  9.5 0.2 reduce-window.8
  9.7 1.1 convert_reduce_fusion.4
  10.9 1.2 multiply_reduce_fusion.5
  12.1 77.9 %all-gather.9.cloned.1.call-done = bf16[3,1408,704]{2,1,0:T(8,128)(2,1)} async-done(((bf16[3,176,704]{2,1,0:T(8,128)(2,1)}), bf16[3,1408,704]{2,1,0:T(8,128)(2,1)}) %all-gather.9.cloned.1.call-update) | async-done | bytes 5947408 | tf_op jit(solution)/shard_map/all_gather | solution.py:143
  90.0 3.4 fusion.24
  93.4 0.7 pad_maximum_fusion.1
  94.2 73.0 %all-gather.13.cloned.1.call-done = bf16[3,1408,704]{2,1,0:T(8,128)(2,1)} async-done(((bf16[3,176,704]{2,1,0:T(8,128)(2,1)}), bf16[3,1408,704]{2,1,0:T(8,128)(2,1)}) %all-gather.13.cloned.1.call-update) | async-done | bytes 5947408 | tf_op jit(solution)/shard_map/all_gather | solution.py:114
  167.2 5.4 %fusion.12 = bf16[3,128,704]{1,2,0:T(8,128)(2,1)S(1)} fusion(bf16[3,1408,704]{2,1,0:T(8,128)(2,1)} %all-gather.13.cloned.1.call-done, bf16[1,128,1408]{2,1,0:T(8,128)(2,1)S(1)} %copy-done, f32[128]{0:T(128)S(1)} %add_rsqrt_fusion.2, f32[128]{0:T(128)S(1)} %broadcast_multiply_fusion.4), kind=kOutput, calls=%fused_computation.25 | convolution fusion | flops 762257408 | bytes 6849536 | tf_op jit(solution)/shard_map/nr,krc->knc/dot_general | solution.py:111
  172.5 0.7 fusion.62
  173.2 0.8 pad_maximum_fusion
  174.1 1.5 broadcast_in_dim.9
  175.5 3.7 all-to-all-start.1
  179.3 1.4 multiply_sine_fusion
  180.8 0.2 fusion.46
  181.1 0.3 multiply_reduce_fusion.6
  181.4 0.7 dynamic-slice
  182.7 0.3 dynamic-update-slice
  183.0 46.7 %all-reduce = s32[3072]{0:T(1024)S(1)} all-reduce(s32[3072]{0:T(1024)S(1)} %dynamic-update-slice), channel_id=2, replica_groups=mesh['seq'=16,'grp'=2,'dp'=8] {'seq'}, use_global_device_ids=true, to_apply=%add | all-reduce | flops 3072 | bytes 24576
  229.7 2.7 fusion.18
  232.4 3.0 fusion.61
  235.5 1.4 copy.38
  236.9 2.3 copy.39
  239.2 0.6 multiply_reduce_fusion.1
  239.7 0.6 fusion.10
  240.4 0.7 fusion.19
  241.1 0.8 convolution_convert_fusion.1
  241.9 0.9 broadcast_in_dim.10
  242.8 4.5 %all-to-all-start.2 = ((bf16[2,128,1408]{2,1,0:T(8,128)(2,1)}), bf16[2,128,1408]{2,1,0:T(8,128)(2,1)}, u32[]{:S(2)}, u32[]{:S(2)}) async-start(bf16[2,128,1408]{2,1,0:T(8,128)(2,1)} %broadcast_in_dim.10), calls=%async_computation.2 | async-start | bytes 1441792 | tf_op jit(solution)/shard_map/all_to_all | solution.py:24
  247.3 0.3 convert_reduce_fusion.1
  247.6 1.0 copy.41
  248.8 2.2 multiply_sine_fusion.1
  251.0 4.2 %all-to-all-done.2 = bf16[2,128,1408]{2,1,0:T(8,128)(2,1)} async-done(((bf16[2,128,1408]{2,1,0:T(8,128)(2,1)}), bf16[2,128,1408]{2,1,0:T(8,128)(2,1)}, u32[]{:S(2)}, u32[]{:S(2)}) %all-to-all-start.2) | async-done | bytes 720928 | tf_op jit(solution)/shard_map/all_to_all | solution.py:24
  255.2 1.3 convert_reduce_fusion.3
  256.5 0.8 copy-done.3
  257.4 1.2 copy.40
  258.6 1.6 fusion.58
  260.2 2.5 all-gather.15.cloned.1.call-done
  262.7 3.2 fusion.60
  265.9 1.4 multiply_reduce_fusion
  267.3 1.6 fusion
  269.0 1.7 fusion.33
  270.7 0.5 convolution_convert_fusion
  271.2 0.9 broadcast_in_dim.11
  272.2 4.3 %all-to-all-start.3 = ((bf16[2,128,1408]{2,1,0:T(8,128)(2,1)}), bf16[2,128,1408]{2,1,0:T(8,128)(2,1)}, u32[]{:S(2)}, u32[]{:S(2)}) async-start(bf16[2,128,1408]{2,1,0:T(8,128)(2,1)} %broadcast_in_dim.11), calls=%async_computation.3 | async-start | bytes 1441792 | tf_op jit(solution)/shard_map/all_to_all | solution.py:24
  276.5 0.2 multiply_reduce_fusion.4
  276.7 8.6 %all-to-all-done.3 = bf16[2,128,1408]{2,1,0:T(8,128)(2,1)} async-done(((bf16[2,128,1408]{2,1,0:T(8,128)(2,1)}), bf16[2,128,1408]{2,1,0:T(8,128)(2,1)}, u32[]{:S(2)}, u32[]{:S(2)}) %all-to-all-start.3) | async-done | bytes 720928 | tf_op jit(solution)/shard_map/all_to_all | solution.py:24
  285.3 1.3 broadcast_in_dim.8
  286.6 4.3 %all-to-all-start = ((bf16[8,128,704]{1,2,0:T(8,128)(2,1)}), bf16[8,128,704]{1,2,0:T(8,128)(2,1)}, u32[]{:S(2)}, u32[]{:S(2)}) async-start(bf16[8,128,704]{1,2,0:T(8,128)(2,1)} %broadcast_in_dim.8), calls=%async_computation | async-start | bytes 2883584 | tf_op jit(solution)/shard_map/all_to_all | solution.py:24
  291.0 1.3 convert_reduce_fusion.2
  292.4 1.1 copy.42
  293.6 0.2 multiply_reduce_fusion.3
  293.8 1.7 fusion.39
  295.6 0.4 multiply_convert_fusion
  296.0 14.9 %all-to-all-done = bf16[8,128,704]{1,2,0:T(8,128)(2,1)} async-done(((bf16[8,128,704]{1,2,0:T(8,128)(2,1)}), bf16[8,128,704]{1,2,0:T(8,128)(2,1)}, u32[]{:S(2)}, u32[]{:S(2)}) %all-to-all-start) | async-done | bytes 1441824 | tf_op jit(solution)/shard_map/all_to_all | solution.py:24
  310.9 9.1 %all_to_all.33 = bf16[128,8,176]{0,2,1:T(8,128)(2,1)S(1)} all-to-all(bf16[128,8,176]{0,2,1:T(8,128)(2,1)S(1)} %multiply_convert_fusion), channel_id=1, replica_groups=mesh['seq'=16,'grp'=2,'dp'=8] {'dp'}, dimensions={1} | all-to-all | bytes 720896 | tf_op jit(solution)/shard_map/all_to_all | solution.py:167
  320.0 2.7 fusion.20
  322.7 4.0 %copy.43 = bf16[704,1408]{0,1:T(8,128)(2,1)} copy(bf16[704,1408]{1,0:T(8,128)(2,1)} %param.12) | data formatting | bytes 3964928 | tf_op args[4]
  326.6 4.4 %multiply_add_fusion = f32[704,1408]{0,1:T(8,128)} fusion(bf16[704,1408]{0,1:T(8,128)(2,1)} %copy.43, bf16[8,704,176]{1,2,0:T(8,128)(2,1)S(1)} %all-to-all-done.1), kind=kLoop, calls=%fused_computation.7 | loop fusion | flops 4956160 | bytes 7929856 | tf_op jit(solution)/shard_map/add | solution.py:176
  331.0 5.6 %copy.44 = f32[704,1408]{1,0:T(8,128)} copy(f32[704,1408]{0,1:T(8,128)} %multiply_add_fusion) | data formatting | bytes 7929856
  336.6 31.9 %all-gather.17.cloned.1.call-done = bf16[16,704,176]{1,2,0:T(8,128)(2,1)} async-done(((bf16[1,704,176]{1,2,0:T(8,128)(2,1)}), bf16[16,704,176]{1,2,0:T(8,128)(2,1)}) %all-gather.17.cloned.1.call-update) | async-done | bytes 3964944 | tf_op jit(solution)/shard_map/all_gather | solution.py:42
  368.5 3.8 convert_reduce_fusion
  (64 shorter events, 0.9 us)
Async XLA Ops:
  7.2 82.8 %all-gather.9.cloned.1.call-start = ((), (), s32[]{:S(2)}) async-start(), calls=%async_computation.5 | async-start | bytes 7299072 | tf_op jit(solution)/shard_map/all_gather | solution.py:143
  7.9 159.3 %all-gather.13.cloned.1.call-start = ((), (), s32[]{:S(2)}) async-start(), calls=%async_computation.7 | async-start | bytes 7299072 | tf_op jit(solution)/shard_map/all_gather | solution.py:114
  8.6 223.8 %all-gather.11.cloned.1.call-start = ((), (), s32[]{:S(2)}) async-start(), calls=%async_computation.6 | async-start | bytes 1531904 | tf_op jit(solution)/shard_map/all_gather | solution.py:19
  12.1 155.1 %copy-start = (bf16[1,128,1408]{2,1,0:T(8,128)(2,1)S(1)}, bf16[1,128,1408]{2,1,0:T(8,128)(2,1)}, u32[]{:S(2)}) copy-start(bf16[1,128,1408]{2,1,0:T(8,128)(2,1)} %param.8) | copy-start | bytes 1081348
  94.1 79.9 %copy-start.13 = (bf16[704,176]{0,1:T(8,128)(2,1)S(1)}, bf16[704,176]{0,1:T(8,128)(2,1)}, u32[]{:S(2)}) copy-start(bf16[704,176]{0,1:T(8,128)(2,1)} %param.14) | copy-start | bytes 743428
  94.1 168.5 %all-gather.15.cloned.1.call-start = ((), (), s32[]{:S(2)}) async-start(), calls=%async_computation.8 | async-start | bytes 6127616 | tf_op jit(solution)/shard_map/all_gather | solution.py:19
  175.5 5.3 %copy-start.14 = (f32[1408]{0:T(1024)S(1)}, f32[1408]{0:T(1024)}, u32[]{:S(2)}) copy-start(f32[1408]{0:T(1024)} %param.15) | copy-start | bytes 16900
  175.5 5.8 %copy-start.16 = (u32[256]{0:T(256)S(1)}, u32[256]{0:T(256)}, u32[]{:S(2)}) copy-start(u32[256]{0:T(256)} %constant.56) | copy-start | bytes 3076
  175.5 7.2 %copy-start.15 = (s32[1,192]{1,0:T(1,128)S(1)}, s32[1,192]{1,0:T(1,128)}, u32[]{:S(2)}) copy-start(s32[1,192]{1,0:T(1,128)} %param.10) | copy-start | bytes 2308
  175.5 65.5 %all-to-all-start.1 = ((bf16[8,704,176]{1,2,0:T(8,128)(2,1)}), bf16[8,704,176]{1,2,0:T(8,128)(2,1)S(1)}, u32[]{:S(2)}, u32[]{:S(2)}) async-start(bf16[8,704,176]{1,2,0:T(8,128)(2,1)} %broadcast_in_dim.9), calls=%async_computation.1 | async-start | bytes 4325376 | tf_op jit(solution)/shard_map/all_to_all | solution.py:24
  180.8 54.7 %copy-start.4 = (f32[128,704]{1,0:T(8,128)}, f32[128,704]{1,0:T(8,128)S(1)}, u32[]{:S(2)}) copy-start(f32[128,704]{1,0:T(8,128)S(1)} %get-tuple-element.23) | copy-start | bytes 1081348
  180.8 54.7 %copy-start.5 = (f32[128,704]{1,0:T(8,128)}, f32[128,704]{1,0:T(8,128)S(1)}, u32[]{:S(2)}) copy-start(f32[128,704]{1,0:T(8,128)S(1)} %get-tuple-element.24) | copy-start | bytes 1081348
  239.2 1.2 copy-start.11
  242.8 12.4 %all-to-all-start.2 = ((bf16[2,128,1408]{2,1,0:T(8,128)(2,1)}), bf16[2,128,1408]{2,1,0:T(8,128)(2,1)}, u32[]{:S(2)}, u32[]{:S(2)}) async-start(bf16[2,128,1408]{2,1,0:T(8,128)(2,1)} %broadcast_in_dim.10), calls=%async_computation.2 | async-start | bytes 1441792 | tf_op jit(solution)/shard_map/all_to_all | solution.py:24
  256.5 0.9 copy-start.3
  260.2 16.3 %copy-start.2 = (f32[128,1408]{1,0:T(8,128)}, f32[128,1408]{1,0:T(8,128)S(1)}, u32[]{:S(2)}) copy-start(f32[128,1408]{1,0:T(8,128)S(1)} %get-tuple-element.11) | copy-start | bytes 2162692
  262.7 3.2 copy-start.12
  269.0 1.8 copy-start.1
  272.2 13.2 %all-to-all-start.3 = ((bf16[2,128,1408]{2,1,0:T(8,128)(2,1)}), bf16[2,128,1408]{2,1,0:T(8,128)(2,1)}, u32[]{:S(2)}, u32[]{:S(2)}) async-start(bf16[2,128,1408]{2,1,0:T(8,128)(2,1)} %broadcast_in_dim.11), calls=%async_computation.3 | async-start | bytes 1441792 | tf_op jit(solution)/shard_map/all_to_all | solution.py:24
  286.6 24.2 %all-to-all-start = ((bf16[8,128,704]{1,2,0:T(8,128)(2,1)}), bf16[8,128,704]{1,2,0:T(8,128)(2,1)}, u32[]{:S(2)}, u32[]{:S(2)}) async-start(bf16[8,128,704]{1,2,0:T(8,128)(2,1)} %broadcast_in_dim.8), calls=%async_computation | async-start | bytes 2883584 | tf_op jit(solution)/shard_map/all_to_all | solution.py:24
  290.9 77.6 %all-gather.17.cloned.1.call-start = ((), (), s32[]{:S(2)}) async-start(), calls=%async_computation.9 | async-start | bytes 4595712 | tf_op jit(solution)/shard_map/all_gather | solution.py:42
  293.6 2.0 copy-start.6
  293.6 2.0 copy-start.7
  293.6 2.0 copy-start.8
  293.6 2.0 copy-start.9
  293.6 2.0 copy-start.10
Sparse Core Ops, SparseCore 0:
  9.8 80.1 all-gather.8
  91.8 75.3 all-gather.12
  169.0 38.1 all-gather.10
  208.8 53.8 all-gather.14
  322.8 45.6 all-gather.16
where the time goes:
time: 380 us; the launch traced here: 379 us
  waiting for transfers between devices  214 us (56%)
  blocking collectives  55.8 us (15%)
  local copies, waits for them, and re-layouts  30.3 us (8%)
  other arithmetic  26.6 us (7%)
  matrix products  19.8 us (5%)
  starting transfers between devices  17 us (4%)
  between operations  14.9 us (4%)
    all_gather x1, waiting for transfers between devices, body(): shard_rows = lax.all_gather(student_qkv, 'dp', axis=1, tiled=True)  77.9 us
    all_gather x1, waiting for transfers between devices, body(): lax.all_gather(target_qkv, 'dp', axis=1, tiled=True)  73 us
    unnamed x1, blocking collectives  46.7 us
    all_gather x1, waiting for transfers between devices, total_of_pieces(): return lax.all_gather(shard, axis).astype(jnp.float32).sum(0)  31.9 us
    all_to_all x4, waiting for transfers between devices, from_everyone(): return lax.all_to_all(copies, axis, split_axis=0, concat_axis=0, tiled=True)  27.7 us
    all_to_all x4, starting transfers between devices, from_everyone(): return lax.all_to_all(copies, axis, split_axis=0, concat_axis=0, tiled=True)  16.8 us
    unnamed x39, local copies, waits for them, and re-layouts  11.5 us
    split x4, local copies, waits for them, and re-layouts, side_by_side(): jnp.split(lax.all_gather(both, axis, axis=dim, tiled=True), ends, axis=al...  9.96 us
  transfers between devices with their start and end apart: 9, of which 7 were waited for; matrix products, arithmetic and copies ran while one was open for 15% of the time, Pallas kernels for 0%

commit v1 on v0

--- a/solution.py
+++ b/solution.py
@@ -111,7 +111,9 @@
     projected = jnp.einsum(
         "nr,krc->knc",
         normed,
-        lax.all_gather(target_qkv, "dp", axis=1, tiled=True),
+        jnp.concatenate(
+            lax.all_to_all(jnp.stack([target_qkv] * lax.axis_size("dp")), "dp", 0, 0), axis=1
+        ),
         preferred_element_type=jnp.float32,
     )
     projected = projected.astype(jnp.bfloat16)

time: 380 us -> 399 us (1.050)
  starting transfers between devices: 17 us -> 25.9 us
  blocking collectives: 55.8 us -> 63.4 us
  local copies, waits for them, and re-layouts: 30.3 us -> 37.9 us
    all_gather x1, waiting for transfers between devices: 77.9 us -> 156 us  [body(): shard_rows = lax.all_gather(student_qkv, 'dp', axis=1, tiled=True)]
    all_gather x1 -> x0, waiting for transfers between devices: 73 us -> none  [body(): lax.all_gather(target_qkv, 'dp', axis=1, tiled=True)]
    unnamed x1, blocking collectives: 46.7 us -> 52.8 us
    all_to_all x0 -> x1, starting transfers between devices: none -> 5.98 us  [body(): lax.all_to_all(jnp.stack([target_qkv] * lax.axis_size('dp')), 'dp', 0, 0)]
    another operation x1 -> x2, local copies, waits for them, and re-layouts: 0.11 us -> 4.33 us  [the longest x1 4.21 us: body(): jnp.stack([target_qkv] * lax.axis_size('dp'))]
    unnamed x39 -> x41, local copies, waits for them, and re-layouts: 11.5 us -> 11.4 us
  transfers between devices with their start and end apart: 9 -> 9, of which waited for: 7 -> 5; matrix products, arithmetic and copies ran while one was open for 15% -> 15% of each run, Pallas kernels for 0% -> 0%
where the time goes in v1:
time: 399 us; the launch traced here: 398 us
  waiting for transfers between devices  215 us (54%)
  blocking collectives  63.4 us (16%)
  local copies, waits for them, and re-layouts  37.9 us (9%)
  starting transfers between devices  25.9 us (6%)
  other arithmetic  23.9 us (6%)
  matrix products  17 us (4%)
  between operations  14.8 us (4%)
    all_gather x1, waiting for transfers between devices, body(): shard_rows = lax.all_gather(student_qkv, 'dp', axis=1, tiled=True)  156 us
    unnamed x1, blocking collectives  52.8 us
    all_gather x1, waiting for transfers between devices, total_of_pieces(): return lax.all_gather(shard, axis).astype(jnp.float32).sum(0)  33.4 us
    all_to_all x4, waiting for transfers between devices, from_everyone(): return lax.all_to_all(copies, axis, split_axis=0, concat_axis=0, tiled=True)  25 us
    all_to_all x4, starting transfers between devices, from_everyone(): return lax.all_to_all(copies, axis, split_axis=0, concat_axis=0, tiled=True)  19.5 us
    unnamed x41, local copies, waits for them, and re-layouts  11.4 us
    all_to_all x1, blocking collectives, body(): lax.all_to_all(back_grad.astype(jnp.bfloat16), 'dp', split_axis=1, concat...  10.6 us
    split x4, local copies, waits for them, and re-layouts, side_by_side(): jnp.split(lax.all_gather(both, axis, axis=dim, tiled=True), ends, axis=al...  10.1 us
  transfers between devices with their start and end apart: 9, of which 5 were waited for; matrix products, arithmetic and copies ran while one was open for 15% of the time, Pallas kernels for 0%

profile of v1, /device:TPU:1, one launch (start us, length us, event | category | flops | bytes accessed | tf_op | source)
XLA Modules:
  0.0 397.8 jit_solution(11555283631176557462)
XLA Ops:
  7.2 0.7 all-gather.8.cloned.1.call-update
  7.9 4.2 %stack.2 = bf16[8,3,176,704]{3,2,1,0:T(8,128)(2,1)} broadcast(bf16[3,176,704]{2,1,0:T(8,128)(2,1)} %param.11), dimensions={1,2,3} | broadcast | bytes 6690816 | tf_op jit(solution)/shard_map/stack | solution.py:115
  12.1 6.0 %all-to-all-start.3 = ((bf16[8,3,176,704]{3,2,1,0:T(8,128)(2,1)}), bf16[8,3,176,704]{3,2,1,0:T(8,128)(2,1)}, u32[]{:S(2)}, u32[]{:S(2)}) async-start(bf16[8,3,176,704]{3,2,1,0:T(8,128)(2,1)} %stack.2), calls=%async_computation.3 | async-start | bytes 12976128 | tf_op jit(solution)/shard_map/all_to_all | solution.py:115
  18.3 0.2 reduce-window.8
  18.7 0.2 multiply_reduce_fusion.5
  19.0 155.7 %all-gather.8.cloned.1.call-done = bf16[3,1408,704]{2,1,0:T(8,128)(2,1)} async-done(((bf16[3,176,704]{2,1,0:T(8,128)(2,1)}), bf16[3,1408,704]{2,1,0:T(8,128)(2,1)}) %all-gather.8.cloned.1.call-update) | async-done | bytes 5947408 | tf_op jit(solution)/shard_map/all_gather | solution.py:145
  174.7 3.3 fusion.24
  178.0 0.7 pad_maximum_fusion.1
  178.8 3.3 copy.46
  182.1 2.6 fusion.12
  184.7 0.7 fusion.69
  185.4 0.8 pad_maximum_fusion
  186.2 1.5 broadcast_in_dim.9
  187.7 6.1 %all-to-all-start.1 = ((bf16[8,704,176]{1,2,0:T(8,128)(2,1)}), bf16[8,704,176]{1,2,0:T(8,128)(2,1)S(1)}, u32[]{:S(2)}, u32[]{:S(2)}) async-start(bf16[8,704,176]{1,2,0:T(8,128)(2,1)} %broadcast_in_dim.9), calls=%async_computation.1 | async-start | bytes 4325376 | tf_op jit(solution)/shard_map/all_to_all | solution.py:24
  193.8 1.4 multiply_sine_fusion
  195.3 0.2 fusion.53
  195.6 0.3 multiply_reduce_fusion.6
  195.9 0.6 dynamic-slice
  197.2 0.3 dynamic-update-slice
  197.4 52.8 %all-reduce = s32[3072]{0:T(1024)S(1)} all-reduce(s32[3072]{0:T(1024)S(1)} %dynamic-update-slice), channel_id=2, replica_groups=mesh['seq'=16,'grp'=2,'dp'=8] {'seq'}, use_global_device_ids=true, to_apply=%add | all-reduce | flops 3072 | bytes 24576
  250.2 2.7 fusion.18
  253.0 3.0 fusion.68
  256.0 1.4 copy.42
  257.4 2.3 copy.43
  259.7 0.6 multiply_reduce_fusion.1
  260.2 0.6 fusion.10
  260.8 0.7 fusion.19
  261.5 0.8 convolution_convert_fusion.1
  262.4 0.9 broadcast_in_dim.10
  263.3 4.3 %all-to-all-start.2 = ((bf16[2,128,1408]{2,1,0:T(8,128)(2,1)}), bf16[2,128,1408]{2,1,0:T(8,128)(2,1)}, u32[]{:S(2)}, u32[]{:S(2)}) async-start(bf16[2,128,1408]{2,1,0:T(8,128)(2,1)} %broadcast_in_dim.10), calls=%async_computation.2 | async-start | bytes 1441792 | tf_op jit(solution)/shard_map/all_to_all | solution.py:24
  267.6 0.3 convert_reduce_fusion.1
  267.9 1.1 copy.45
  269.0 2.2 multiply_sine_fusion.1
  271.2 4.4 %all-to-all-done.2 = bf16[2,128,1408]{2,1,0:T(8,128)(2,1)} async-done(((bf16[2,128,1408]{2,1,0:T(8,128)(2,1)}), bf16[2,128,1408]{2,1,0:T(8,128)(2,1)}, u32[]{:S(2)}, u32[]{:S(2)}) %all-to-all-start.2) | async-done | bytes 720928 | tf_op jit(solution)/shard_map/all_to_all | solution.py:24
  275.6 1.3 convert_reduce_fusion.3
  276.9 0.8 copy-done.3
  277.8 1.1 copy.44
  278.9 1.6 fusion.65
  280.6 3.4 fusion.67
  284.0 1.4 multiply_reduce_fusion
  285.4 1.6 fusion
  287.1 1.7 fusion.33
  288.8 0.5 convolution_convert_fusion
  289.4 0.9 broadcast_in_dim.11
  290.3 4.3 %all-to-all-start.4 = ((bf16[2,128,1408]{2,1,0:T(8,128)(2,1)}), bf16[2,128,1408]{2,1,0:T(8,128)(2,1)}, u32[]{:S(2)}, u32[]{:S(2)}) async-start(bf16[2,128,1408]{2,1,0:T(8,128)(2,1)} %broadcast_in_dim.11), calls=%async_computation.4 | async-start | bytes 1441792 | tf_op jit(solution)/shard_map/all_to_all | solution.py:24
  294.6 0.2 multiply_reduce_fusion.4
  294.8 7.8 %all-to-all-done.4 = bf16[2,128,1408]{2,1,0:T(8,128)(2,1)} async-done(((bf16[2,128,1408]{2,1,0:T(8,128)(2,1)}), bf16[2,128,1408]{2,1,0:T(8,128)(2,1)}, u32[]{:S(2)}, u32[]{:S(2)}) %all-to-all-start.4) | async-done | bytes 720928 | tf_op jit(solution)/shard_map/all_to_all | solution.py:24
  302.6 1.3 broadcast_in_dim.8
  303.9 4.9 %all-to-all-start = ((bf16[8,128,704]{1,2,0:T(8,128)(2,1)}), bf16[8,128,704]{1,2,0:T(8,128)(2,1)}, u32[]{:S(2)}, u32[]{:S(2)}) async-start(bf16[8,128,704]{1,2,0:T(8,128)(2,1)} %broadcast_in_dim.8), calls=%async_computation | async-start | bytes 2883584 | tf_op jit(solution)/shard_map/all_to_all | solution.py:24
  308.8 0.3 all-gather.14.cloned.1.call-start
  309.1 1.3 convert_reduce_fusion.2
  310.4 0.2 fusion.51
  310.5 1.1 copy.48
  311.7 0.2 multiply_reduce_fusion.3
  312.0 1.7 fusion.39
  313.7 0.4 multiply_convert_fusion
  314.1 12.7 %all-to-all-done = bf16[8,128,704]{1,2,0:T(8,128)(2,1)} async-done(((bf16[8,128,704]{1,2,0:T(8,128)(2,1)}), bf16[8,128,704]{1,2,0:T(8,128)(2,1)}, u32[]{:S(2)}, u32[]{:S(2)}) %all-to-all-start) | async-done | bytes 1441824 | tf_op jit(solution)/shard_map/all_to_all | solution.py:24
  326.8 10.6 %all_to_all.38 = bf16[128,8,176]{0,2,1:T(8,128)(2,1)S(1)} all-to-all(bf16[128,8,176]{0,2,1:T(8,128)(2,1)S(1)} %multiply_convert_fusion), channel_id=1, replica_groups=mesh['seq'=16,'grp'=2,'dp'=8] {'dp'}, dimensions={1} | all-to-all | bytes 720896 | tf_op jit(solution)/shard_map/all_to_all | solution.py:169
  337.4 2.7 fusion.20
  340.1 4.0 copy.49
  344.0 4.4 %multiply_add_fusion = f32[704,1408]{0,1:T(8,128)} fusion(bf16[704,1408]{0,1:T(8,128)(2,1)} %copy.49, bf16[8,704,176]{1,2,0:T(8,128)(2,1)S(1)} %all-to-all-done.1), kind=kLoop, calls=%fused_computation.7 | loop fusion | flops 4956160 | bytes 7929856 | tf_op jit(solution)/shard_map/add | solution.py:178
  348.4 5.6 %copy.50 = f32[704,1408]{1,0:T(8,128)} copy(f32[704,1408]{0,1:T(8,128)} %multiply_add_fusion) | data formatting | bytes 7929856
  354.0 33.4 %all-gather.14.cloned.1.call-done = bf16[16,704,176]{1,2,0:T(8,128)(2,1)} async-done(((bf16[1,704,176]{1,2,0:T(8,128)(2,1)}), bf16[16,704,176]{1,2,0:T(8,128)(2,1)}) %all-gather.14.cloned.1.call-update) | async-done | bytes 3964944 | tf_op jit(solution)/shard_map/all_gather | solution.py:42
  387.5 3.8 convert_reduce_fusion
  (67 shorter events, 0.8 us)
Async XLA Ops:
  7.2 167.5 %all-gather.8.cloned.1.call-start = ((), (), s32[]{:S(2)}) async-start(), calls=%async_computation.6 | async-start | bytes 7299072 | tf_op jit(solution)/shard_map/all_gather | solution.py:145
  12.1 6.0 %copy-start.16 = (s32[1,128]{1,0:T(1,128)S(1)}, s32[1,128]{1,0:T(1,128)}, u32[]{:S(2)}) copy-start(s32[1,128]{1,0:T(1,128)} %param.9) | copy-start | bytes 1540
  12.1 6.4 %copy-start = (bf16[1,128,1408]{2,1,0:T(8,128)(2,1)S(1)}, bf16[1,128,1408]{2,1,0:T(8,128)(2,1)}, u32[]{:S(2)}) copy-start(bf16[1,128,1408]{2,1,0:T(8,128)(2,1)} %param.8) | copy-start | bytes 1081348
  12.1 166.6 %all-to-all-start.3 = ((bf16[8,3,176,704]{3,2,1,0:T(8,128)(2,1)}), bf16[8,3,176,704]{3,2,1,0:T(8,128)(2,1)}, u32[]{:S(2)}, u32[]{:S(2)}) async-start(bf16[8,3,176,704]{3,2,1,0:T(8,128)(2,1)} %stack.2), calls=%async_computation.3 | async-start | bytes 12976128 | tf_op jit(solution)/shard_map/all_to_all | solution.py:115
  18.1 234.9 %all-gather.10.cloned.1.call-start = ((), (), s32[]{:S(2)}) async-start(), calls=%async_computation.7 | async-start | bytes 1531904 | tf_op jit(solution)/shard_map/all_gather | solution.py:19
  178.7 101.9 %all-gather.12.cloned.1.call-start = ((), (), s32[]{:S(2)}) async-start(), calls=%async_computation.8 | async-start | bytes 6127616 | tf_op jit(solution)/shard_map/all_gather | solution.py:19
  182.1 4.1 %copy-start.13 = (bf16[704,176]{0,1:T(8,128)(2,1)S(1)}, bf16[704,176]{0,1:T(8,128)(2,1)}, u32[]{:S(2)}) copy-start(bf16[704,176]{0,1:T(8,128)(2,1)} %param.14) | copy-start | bytes 743428
  187.7 7.6 %copy-start.14 = (f32[1408]{0:T(1024)S(1)}, f32[1408]{0:T(1024)}, u32[]{:S(2)}) copy-start(f32[1408]{0:T(1024)} %param.15) | copy-start | bytes 16900
  187.7 8.1 %copy-start.17 = (u32[256]{0:T(256)S(1)}, u32[256]{0:T(256)}, u32[]{:S(2)}) copy-start(u32[256]{0:T(256)} %constant.56) | copy-start | bytes 3076
  187.7 9.4 %copy-start.15 = (s32[1,192]{1,0:T(1,128)S(1)}, s32[1,192]{1,0:T(1,128)}, u32[]{:S(2)}) copy-start(s32[1,192]{1,0:T(1,128)} %param.10) | copy-start | bytes 2308
  187.7 73.8 %all-to-all-start.1 = ((bf16[8,704,176]{1,2,0:T(8,128)(2,1)}), bf16[8,704,176]{1,2,0:T(8,128)(2,1)S(1)}, u32[]{:S(2)}, u32[]{:S(2)}) async-start(bf16[8,704,176]{1,2,0:T(8,128)(2,1)} %broadcast_in_dim.9), calls=%async_computation.1 | async-start | bytes 4325376 | tf_op jit(solution)/shard_map/all_to_all | solution.py:24
  195.3 60.7 %copy-start.4 = (f32[128,704]{1,0:T(8,128)}, f32[128,704]{1,0:T(8,128)S(1)}, u32[]{:S(2)}) copy-start(f32[128,704]{1,0:T(8,128)S(1)} %get-tuple-element.23) | copy-start | bytes 1081348
  195.3 60.7 %copy-start.5 = (f32[128,704]{1,0:T(8,128)}, f32[128,704]{1,0:T(8,128)S(1)}, u32[]{:S(2)}) copy-start(f32[128,704]{1,0:T(8,128)S(1)} %get-tuple-element.24) | copy-start | bytes 1081348
  259.7 1.2 copy-start.11
  263.3 12.4 %all-to-all-start.2 = ((bf16[2,128,1408]{2,1,0:T(8,128)(2,1)}), bf16[2,128,1408]{2,1,0:T(8,128)(2,1)}, u32[]{:S(2)}, u32[]{:S(2)}) async-start(bf16[2,128,1408]{2,1,0:T(8,128)(2,1)} %broadcast_in_dim.10), calls=%async_computation.2 | async-start | bytes 1441792 | tf_op jit(solution)/shard_map/all_to_all | solution.py:24
  276.9 0.9 copy-start.3
  280.5 14.0 %copy-start.2 = (f32[128,1408]{1,0:T(8,128)}, f32[128,1408]{1,0:T(8,128)S(1)}, u32[]{:S(2)}) copy-start(f32[128,1408]{1,0:T(8,128)S(1)} %get-tuple-element.11) | copy-start | bytes 2162692
  280.6 3.5 copy-start.12
  287.1 1.8 copy-start.1
  290.3 12.4 %all-to-all-start.4 = ((bf16[2,128,1408]{2,1,0:T(8,128)(2,1)}), bf16[2,128,1408]{2,1,0:T(8,128)(2,1)}, u32[]{:S(2)}, u32[]{:S(2)}) async-start(bf16[2,128,1408]{2,1,0:T(8,128)(2,1)} %broadcast_in_dim.11), calls=%async_computation.4 | async-start | bytes 1441792 | tf_op jit(solution)/shard_map/all_to_all | solution.py:24
  303.9 22.9 %all-to-all-start = ((bf16[8,128,704]{1,2,0:T(8,128)(2,1)}), bf16[8,128,704]{1,2,0:T(8,128)(2,1)}, u32[]{:S(2)}, u32[]{:S(2)}) async-start(bf16[8,128,704]{1,2,0:T(8,128)(2,1)} %broadcast_in_dim.8), calls=%async_computation | async-start | bytes 2883584 | tf_op jit(solution)/shard_map/all_to_all | solution.py:24
  308.8 78.7 %all-gather.14.cloned.1.call-start = ((), (), s32[]{:S(2)}) async-start(), calls=%async_computation.9 | async-start | bytes 4595712 | tf_op jit(solution)/shard_map/all_gather | solution.py:42
  311.7 2.0 copy-start.6
  311.7 2.0 copy-start.7
  311.7 2.0 copy-start.8
  311.7 2.0 copy-start.9
  311.7 2.0 copy-start.10
Sparse Core Ops, SparseCore 0:
  9.8 164.8 all-gather.7
  178.8 45.8 all-gather.9
  226.5 53.2 all-gather.11
  340.2 47.2 all-gather.13
